TPU v7x, 32 devices: a whole 2x2x4 slice. The times are simulated.
32 devices in a mesh: dp: 16 (over z, y, core), tensor: 2 (over x).
Axes of the slice: x: 2, y: 2, z: 4, core: 2. Of those that a mesh axis runs over, the one named last changes fastest.
Arguments:
- training_token_input: bfloat16 [4096, 8192], P('dp', 'tensor'), may hold values from -6 to 6
- gate_output_gradient: bfloat16 [4096, 29568], P('dp', 'tensor'), may hold values from -6 to 6
- up_output_gradient: bfloat16 [4096, 29568], P('dp', 'tensor'), may hold values from -6 to 6
- gate_first_matrix: bfloat16 [8192, 64], P('tensor'), may hold values from -0.0625 to 0.0625
- gate_second_matrix: bfloat16 [64, 29568], P(None, 'tensor'), may hold values from -0.75 to 0.75
- up_first_matrix: bfloat16 [8192, 64], P('tensor'), may hold values from -0.0625 to 0.0625
- up_second_matrix: bfloat16 [64, 29568], P(None, 'tensor'), may hold values from -0.75 to 0.75
- gate_weight_base: bfloat16 [8192, 29568], P('tensor', 'dp'), may hold values from -0.0625 to 0.0625
- up_weight_base: bfloat16 [8192, 29568], P('tensor', 'dp'), may hold values from -0.0625 to 0.0625
- down_weight_base: bfloat16 [29568, 8192], P('dp', 'tensor'), may hold values from -0.03125 to 0.03125
- decode_step_input: bfloat16 [2, 512, 8192], P(None, None, 'tensor'), may hold values from -6 to 6
Outputs:
- decoded: bfloat16 [2, 512, 8192], P(None, None, 'tensor')
All inputs are finite; a program needn't handle non-finite values.
Results may differ from a plain program's by a relative error of at most 0.04.
Values may be sent and summed in bfloat16 or wider, within the bound.
A program may use at most 192 MiB of HBM per device.

v0:
```python
import functools
import math

import jax
import jax.numpy as jnp
from jax import lax
from jax.experimental import pallas as pl
from jax.experimental.pallas import tpu as pltpu
from jax.sharding import PartitionSpec as P

MODEL_WIDTH = 8192
HIDDEN_UNITS = 29568
ADAPTER_RANK = 64
MESH = pl.DeviceIdType.MESH
F32, BF16 = jnp.float32, jnp.bfloat16


def swap(value):
    return lax.ppermute(value, "tensor", ((0, 1), (1, 0)))


def pair_sum(value):
    if lax.axis_size("tensor") == 2:
        sent = value.astype(jnp.bfloat16)
        return sent.astype(jnp.float32) + swap(sent).astype(jnp.float32)
    return lax.psum(value.astype(jnp.bfloat16), "tensor").astype(jnp.float32)


def row_share(value, index):
    rows = value.shape[1] // lax.axis_size("tensor")
    return lax.dynamic_slice_in_dim(value, index * rows, rows, 1)


class Place:
    def __init__(self, n_dp):
        self.chips = n_dp // 2
        depth = self.chips // 2
        dp = lax.axis_index("dp")
        self.t = lax.axis_index("tensor")
        self.core = lax.rem(dp, 2)
        y = lax.rem(dp // 2, 2)
        z = dp // 4
        where = jnp.where(y == 0, z, self.chips - 1 - z)
        self.turn = jnp.where(self.core == 0, where, lax.rem(self.chips - where, self.chips))

        def chip(position):
            position = lax.rem(position + self.chips, self.chips)
            up = position < depth
            there = jnp.where(up, position * 2, (self.chips - 1 - position) * 2 + 1)
            return (there * 2 + self.core, self.t)

        step = jnp.where(self.core == 0, 1, -1)
        self.after = chip(where + step)
        self.before = chip(where - step)
        self.across = (dp, 1 - self.t)
        self.mate = (dp + 1 - 2 * self.core, self.t)
        self.flips = []
        bit = 1
        while bit < n_dp:
            self.flips.append((dp + bit - 2 * bit * lax.rem(dp // bit, 2), self.t))
            bit *= 2


def remote(src, dst, send, recv, target):
    return pltpu.make_async_remote_copy(
        src_ref=src, dst_ref=dst, send_sem=send, recv_sem=recv, device_id=target, device_id_type=MESH
    )


def greet(targets):
    barrier = pltpu.get_barrier_semaphore()
    for target in targets:
        pl.semaphore_signal(barrier, inc=1, device_id=target, device_id_type=MESH)
    pl.semaphore_wait(barrier, len(targets))


def decode_kernel(
    n_dp, steps, inputs_ref, gate_ref, up_ref, down_ref, low_ref, pass_ref, second_ref, first_gate_ref, first_up_ref, out_ref,
    source, piece, own, sent, come, low, passing, passed, second, weight, rows, keep, give, take, ring, result,
    source_sem, piece_sem, small_sem, weight_sem, store_sem, part_send, part_recv, low_send, low_recv, across_send, across_recv,
    mate_send, mate_recv, sum_send, sum_recv, all_send, all_recv, copy_send, copy_recv,
):
    place = Place(n_dp)
    n = place.chips
    chunks = rows.shape[0]
    per = chunks // steps
    share = source.shape[1]
    part = share // per
    units = rows.shape[2]
    half = weight.shape[1] // 2
    shard = 2 * part // n
    tile = min(512, half)
    tiles = half // tile
    spans = [(i, min(piece.shape[1], units - i)) for i in range(0, units, piece.shape[1])]
    mine = pl.multiple_of(place.core * half, half)
    other = pl.multiple_of((1 - place.core) * half, half)

    groups = [(0, place.t), (1, 1 - place.t), (1, place.t)]
    turns = [(g, m, span) for g in range(len(groups)) for m in range(2) for span in spans]

    def source_copy(g):
        step, side = groups[g]
        first = pl.multiple_of(step * 2 * share + side * share, share)
        return pltpu.make_async_copy(inputs_ref.at[pl.ds(first, share), :], source.at[g % 2], source_sem.at[g % 2])

    def piece_copy(i):
        _, m, (first, width) = turns[i]
        ref = (gate_ref, up_ref)[m]
        return pltpu.make_async_copy(
            ref.at[pl.ds(first, width), :], piece.at[i % 2, pl.ds(0, width), :], piece_sem.at[i % 2]
        )

    smalls = [
        pltpu.make_async_copy(low_ref, low, small_sem.at[0]),
        pltpu.make_async_copy(second_ref, second, small_sem.at[1]),
        pltpu.make_async_copy(first_gate_ref, come.at[0, 0], small_sem.at[2]),
        pltpu.make_async_copy(first_up_ref, come.at[0, 1], small_sem.at[3]),
        pltpu.make_async_copy(pass_ref, passing, small_sem.at[4]),
    ]
    low_copy = remote(passing, passed, low_send.at[0], low_recv.at[0], place.across)
    weight_load = pltpu.make_async_copy(down_ref, weight, weight_sem.at[0])

    source_copy(0).start()
    piece_copy(0).start()
    piece_copy(1).start()
    source_copy(1).start()
    for small in smalls:
        small.start()
    greet((place.across, place.mate, place.after, place.before))
    for small in smalls:
        small.wait()
    low_copy.start()

    def base(g):
        for i, (group, m, (first, width)) in enumerate(turns):
            if group != g:
                continue
            if m == 0 and first == 0:
                source_copy(g).wait()
            piece_copy(i).wait()
            columns = pl.ds(first, width)
            value = lax.dot_general(
                source[g % 2], piece[i % 2, :width, :], (((1,), (1,)), ((), ())), preferred_element_type=F32
            ).astype(BF16)
            if g == 1:
                sent[m, :, columns] = value
            else:
                own[groups[g][0], m, :, columns] = value
            if i + 2 < len(turns):
                piece_copy(i + 2).start()
            if m == 1 and (first, width) == spans[-1] and g + 2 < len(groups):
                source_copy(g + 2).start()
            yield

    def partial_copies(q):
        here = pl.ds((q % per) * part, part)
        return [
            remote(sent.at[m, here, :], come.at[1, m, here, :], part_send.at[q % per, m], part_recv.at[q % per, m], place.across)
            for m in range(2)
        ]

    def own_rows(q):
        return rows.at[q, pl.ds(pl.multiple_of(place.t * part, part), part), :]

    def crossing(q):
        return remote(own_rows(q), own_rows(q), across_send.at[q], across_recv.at[q], place.across)

    def hidden(q):
        step = q // per
        count = 64
        for i in range(part // count):
            here = pl.ds((q % per) * part + i * count, count)
            line = pl.ds(q * part + i * count, count)
            there = pl.ds(pl.multiple_of(place.t * part + i * count, count), count)
            for first, width in spans:
                columns = pl.ds(first, width)

                def pre(m):
                    return (
                        own[step, m, here, columns].astype(F32) + come[step, m, here, columns].astype(F32)
                        + jnp.dot(low[m, line, :], second[m, :, columns], preferred_element_type=F32)
                    )

                gate = pre(0)
                rows[q, there, columns] = (gate / (1.0 + jnp.exp(-gate)) * pre(1)).astype(BF16)
        crossing(q).start()

    def shard_rows(index):
        index = lax.rem(index + 2 * n, n)
        return pl.ds(pl.multiple_of(index * shard, shard), shard)

    def product(q, i, target, start):
        block = pl.ds(pl.multiple_of(start + i * tile, tile), tile)
        value = jnp.dot(rows[q], weight[:, block], preferred_element_type=F32)
        target[q, :, pl.ds(i * tile, tile)] = value.astype(BF16)

    pending = []

    def project(q):
        crossing(q).wait_recv()
        exchange = remote(give.at[q], take.at[q], mate_send.at[q], mate_recv.at[q], place.mate)
        for i in range(tiles):
            product(q, i, give, other)
            if i == tiles - 1:
                exchange.start()
            yield
        for i in range(tiles):
            product(q, i, keep, mine)
            yield
        exchange.wait()

    up, down = n // 2, n - 1 - n // 2
    ways = ((0, up, place.after), (1, down, place.before))

    def spread(q):
        hops = [None, None]

        def mix(where):
            return keep[q, where, :].astype(F32) + take[q, where, :].astype(F32)

        for s in range(up):
            for d, count, there in ways:
                if s < count:
                    where = shard_rows(place.turn + (up - s if d == 0 else s - down))
                    value = mix(where)
                    if s > 0:
                        hops[d].wait()
                        value = value + ring[q, d * up + s - 1].astype(F32)
                    keep[q, where, :] = value.astype(BF16)
                    slot = d * up + s
                    hops[d] = remote(
                        keep.at[q, where, :], ring.at[q, slot], sum_send.at[q, slot], sum_recv.at[q, slot], there
                    )
                    hops[d].start()
            yield
        where = shard_rows(place.turn)
        value = mix(where)
        for d, count, there in ways:
            hops[d].wait()
            value = value + ring[q, d * up + count - 1].astype(F32)
        result[q, where, pl.ds(mine, half)] = value.astype(BF16)
        copies = []
        for s in range(up + 1):
            for d, count, there in ways:
                if s > count:
                    continue
                if s > 0:
                    hops[d].wait()
                block = result.at[q, shard_rows(place.turn + (-s if d == 0 else s)), pl.ds(mine, half)]
                if s < count:
                    slot = d * up + s
                    hops[d] = remote(block, block, all_send.at[q, slot], all_recv.at[q, slot], there)
                    hops[d].start()
                if s > 0 or d == 0:
                    slot = d * up + s
                    copy = remote(block, block, copy_send.at[q, slot], copy_recv.at[q, slot], place.mate)
                    copy.start()
                    copies.append(copy)
            yield
        for copy in copies:
            copy.wait()
        for side in range(2):
            first = (q // per) * 2 * share + side * share + (q % per) * part
            store = pltpu.make_async_copy(
                result.at[q, pl.ds(side * part, part), :], out_ref.at[pl.ds(first, part), :], store_sem.at[q, side]
            )
            store.start()
            pending.append(store)

    for _ in base(0):
        pass
    weight_load.start()
    low_copy.wait()
    low[...] = (low[...].astype(F32) + passed[...].astype(F32)).astype(BF16)
    hidden(0)
    hidden(1)
    for _ in base(1):
        pass
    for copy in partial_copies(2):
        copy.start()
    weight_load.wait()
    for _ in project(0):
        pass
    live = {0: spread(0)}

    def paced(units, count):
        for i, _ in enumerate(units):
            if i % count == count - 1:
                yield

    def background():
        yield
        for _ in project(1):
            pass
        live[1] = spread(1)
        yield
        yield from paced(base(2), 6)
        for copy in partial_copies(2):
            copy.wait_recv()
        hidden(2)
        for copy in partial_copies(3):
            copy.start()
        yield
        yield
        yield from paced(project(2), 4)
        live[2] = spread(2)
        yield
        yield
        for copy in partial_copies(3):
            copy.wait_recv()
        hidden(3)
        yield
        yield
        for _ in project(3):
            pass
        live[3] = spread(3)

    rest = background()
    busy = True
    while busy or live:
        for q in list(live):
            if next(live[q], live) is live:
                del live[q]
        if busy and next(rest, live) is live:
            busy = False
    for store in pending:
        store.wait()
    for q in range(chunks):
        crossing(q).wait_send()
    for q in range(per, chunks):
        for copy in partial_copies(q):
            copy.wait_send()


def decode(inputs, gate, up, down, low, passing, second, first_gate, first_up, steps):
    n_dp = lax.axis_size("dp")
    n = n_dp // 2
    count, features = inputs.shape
    units, width = down.shape
    chunks = 2 * steps
    share = count // (2 * steps)
    both = count // chunks
    rank = low.shape[2]
    dma = pltpu.SemaphoreType.DMA
    anywhere = pl.BlockSpec(memory_space=pl.ANY)
    return pl.pallas_call(
        functools.partial(decode_kernel, n_dp, steps),
        out_shape=jax.ShapeDtypeStruct((count, width), BF16),
        in_specs=[anywhere] * 9,
        out_specs=anywhere,
        scratch_shapes=[
            pltpu.VMEM((2, share, features), BF16),
            pltpu.VMEM((2, 256, features), BF16),
            pltpu.VMEM((steps, 2, share, units), BF16),
            pltpu.VMEM((2, share, units), BF16),
            pltpu.VMEM((steps, 2, share, units), BF16),
            pltpu.VMEM(low.shape, BF16),
            pltpu.VMEM(low.shape, BF16),
            pltpu.VMEM(low.shape, BF16),
            pltpu.VMEM((2, rank, units), BF16),
            pltpu.VMEM((units, width), BF16),
            pltpu.VMEM((chunks, both, units), BF16),
            pltpu.VMEM((chunks, both, width // 2), BF16),
            pltpu.VMEM((chunks, both, width // 2), BF16),
            pltpu.VMEM((chunks, both, width // 2), BF16),
            pltpu.VMEM((chunks, n - 1, both // n, width // 2), BF16),
            pltpu.VMEM((chunks, both, width), BF16),
            dma((2,)), dma((2,)), dma((5,)), dma((1,)), dma((chunks, 2)),
            dma((2, 2)), dma((2, 2)), dma((1,)), dma((1,)), dma((chunks,)), dma((chunks,)), dma((chunks,)), dma((chunks,)),
            dma((chunks, n)), dma((chunks, n)), dma((chunks, n)), dma((chunks, n)),
            dma((chunks, n)), dma((chunks, n)),
        ],
        compiler_params=pltpu.CompilerParams(
            collective_id=0, has_side_effects=True, vmem_limit_bytes=63 * 1024 * 1024
        ),
        name="decode",
    )(inputs, gate, up, down, low, passing, second, first_gate, first_up)


def seconds_kernel(
    n_dp, n_tensor, rate, gate_ref, up_ref, old_ref, change_ref, out_ref, change_out_ref,
    change, summed, heard, whole, raw, block, take, ring, old, fresh,
    load_sem, old_sem, store_sem, mate_send, mate_recv, ring_send, ring_recv, across_send, across_recv,
    change_sem, hear_send, hear_recv,
):
    place = Place(n_dp)
    n = place.chips
    depth = n // 2
    rank = raw.shape[1]
    units = block.shape[2]
    kept = n // n_tensor
    cuts = ring_send.shape[2]
    cut = 2 * rank // cuts

    loads = [pltpu.make_async_copy(ref, raw.at[p], load_sem.at[p]) for p, ref in enumerate((gate_ref, up_ref))]
    for load in loads:
        load.start()
    held = pltpu.make_async_copy(old_ref, old, old_sem.at[0])
    held.start()
    change_load = pltpu.make_async_copy(change_ref, change, change_sem.at[0])
    change_load.start()
    greet((place.across, place.mate, place.after, place.before) + tuple(place.flips[1:]))
    change_load.wait()
    rounds = len(place.flips)

    lines = heard.shape[1]

    def hear(i):
        if i == 0:
            src = change.at[pl.ds(pl.multiple_of((1 - place.core) * lines, lines), lines), :]
        else:
            src = summed.at[i - 1]
        return remote(src, heard.at[i], hear_send.at[i], hear_recv.at[i], place.flips[i])

    def gather(i):
        hear(i).wait()
        mine = pl.ds(pl.multiple_of(place.core * lines, lines), lines)
        before = change[mine, :] if i == 0 else summed[i - 1]
        value = (before.astype(F32) + heard[i].astype(F32)).astype(BF16)
        if i + 1 < rounds:
            summed[i] = value
            hear(i + 1).start()
        else:
            whole[mine, :] = value

    def complete():
        mine = pl.ds(pl.multiple_of(place.core * lines, lines), lines)
        return remote(whole.at[mine, :], whole.at[mine, :], hear_send.at[rounds], hear_recv.at[rounds], place.mate)

    hear(0).start()
    for load in loads:
        load.wait()

    exchanges = []
    for j in range(kept):
        for k in (2 * j, 2 * j + 1):
            for p in range(2):
                block[k, p * rank : (p + 1) * rank, :] = raw[p, :, k * units : (k + 1) * units]
        exchange = remote(
            block.at[2 * j + 1 - place.core], take.at[j], mate_send.at[j], mate_recv.at[j], place.mate
        )
        exchange.start()
        exchanges.append(exchange)
    gather(0)
    for exchange in exchanges:
        exchange.wait()
    held.wait()

    def target(index):
        index = lax.rem(index + 2 * n, n)
        where = jnp.where(place.core == 0, index, lax.rem(n - index, n))
        y = jnp.where(where < depth, 0, 1)
        z = jnp.where(where < depth, where, n - 1 - where)
        per = depth // n_tensor
        return z // per == place.t, lax.rem(z, per) * 2 + y

    def hop(d, j, u):
        own = pl.ds(u * cut, cut)
        return remote(
            block.at[2 * j + place.core, own, :], ring.at[d, j, own, :],
            ring_send.at[d, j, u], ring_recv.at[d, j, u], (place.after, place.before)[d],
        )

    def final(u):
        own = pl.ds(u * cut, cut)
        return remote(fresh.at[own, :], fresh.at[own, :], across_send.at[u], across_recv.at[u], place.across)

    up, down = n // 2, n - 1 - n // 2
    sends = [
        (s, d, target(place.turn + (up - s if d == 0 else s - down)))
        for s in range(up) for d, count in ((0, up), (1, down)) if s < count
    ]

    def mix(j, u):
        own = pl.ds(u * cut, cut)
        return block[2 * j + place.core, own, :].astype(F32) + take[j, own, :].astype(F32)

    for s, d, (active, j) in sends:

        @pl.when(active)
        def _():
            for u in range(cuts):
                own = pl.ds(u * cut, cut)
                value = mix(j, u)
                if s > 0:
                    hop(d, j, u).wait_recv()
                    value = value + ring[d, j, own, :].astype(F32)
                block[2 * j + place.core, own, :] = value.astype(BF16)
                hop(d, j, u).start()

        if d == 0 and 1 <= s < rounds - 1:
            gather(s)

    owner, j = target(place.turn)

    @pl.when(owner)
    def _():
        for u in range(cuts):
            own = pl.ds(u * cut, cut)
            value = mix(j, u)
            for d in range(2):
                hop(d, j, u).wait_recv()
                value = value + ring[d, j, own, :].astype(F32)
            fresh[own, :] = (old[own, :].astype(F32) - rate * value).astype(BF16)
            final(u).start()

    gather(rounds - 1)
    complete().start()
    for s, d, (active, j) in sends:

        @pl.when(active)
        def _():
            for u in range(cuts):
                hop(d, j, u).wait_send()

    @pl.when(owner)
    def _():
        for u in range(cuts):
            final(u).wait_send()

    @pl.when(jnp.logical_not(owner))
    def _():
        for u in range(cuts):
            final(u).wait_recv()

    complete().wait()
    stores = [
        pltpu.make_async_copy(fresh, out_ref, store_sem.at[0]),
        pltpu.make_async_copy(whole, change_out_ref, change_sem.at[1]),
    ]
    for store in stores:
        store.start()
    for store in stores:
        store.wait()


def new_seconds(gate_gradient, up_gradient, old, change, rate):
    rounds = 4
    n_dp, n_tensor = lax.axis_size("dp"), lax.axis_size("tensor")
    both, units = old.shape
    n = n_dp // 2
    kept, cuts = n // n_tensor, 4
    dma = pltpu.SemaphoreType.DMA
    anywhere = pl.BlockSpec(memory_space=pl.ANY)
    return pl.pallas_call(
        functools.partial(seconds_kernel, n_dp, n_tensor, rate),
        out_shape=(jax.ShapeDtypeStruct((both, units), BF16), jax.ShapeDtypeStruct(change.shape, BF16)),
        in_specs=[anywhere] * 4,
        out_specs=(anywhere, anywhere),
        scratch_shapes=[
            pltpu.VMEM(change.shape, BF16),
            pltpu.VMEM((rounds - 1, change.shape[0] // 2, both), BF16),
            pltpu.VMEM((rounds, change.shape[0] // 2, both), BF16),
            pltpu.VMEM(change.shape, BF16),
            pltpu.VMEM((2, both // 2, gate_gradient.shape[1]), BF16),
            pltpu.VMEM((2 * kept, both, units), BF16),
            pltpu.VMEM((kept, both, units), BF16),
            pltpu.VMEM((2, kept, both, units), BF16),
            pltpu.VMEM((both, units), BF16),
            pltpu.VMEM((both, units), BF16),
            dma((2,)), dma((1,)), dma((1,)),
            dma((kept,)), dma((kept,)), dma((2, kept, cuts)), dma((2, kept, cuts)), dma((cuts,)), dma((cuts,)),
            dma((2,)), dma((rounds + 1,)), dma((rounds + 1,)),
        ],
        compiler_params=pltpu.CompilerParams(
            collective_id=1, has_side_effects=True, vmem_limit_bytes=28 * 1024 * 1024
        ),
        cost_estimate=pl.CostEstimate(flops=0, bytes_accessed=100_000_000, transcendentals=0),
        name="seconds",
    )(gate_gradient, up_gradient, old, change)


def on_device(
    training_token_input,
    gate_output_gradient,
    up_output_gradient,
    gate_first_matrix,
    gate_second_matrix,
    up_first_matrix,
    up_second_matrix,
    gate_weight_base,
    up_weight_base,
    down_weight_base,
    decode_step_input,
):
    f32, bf16 = jnp.float32, jnp.bfloat16
    n_dp, n_tensor = lax.axis_size("dp"), lax.axis_size("tensor")
    me = lax.axis_index("tensor")
    replica = lax.axis_index("dp")
    rank = gate_first_matrix.shape[1]
    tokens_total = training_token_input.shape[0] * n_dp
    second_learning_rate = 0.5 / math.sqrt(ADAPTER_RANK * tokens_total)
    first_learning_rate = 0.5 / math.sqrt(MODEL_WIDTH * HIDDEN_UNITS * tokens_total / ADAPTER_RANK)
    kernels = n_tensor == 2 and n_dp == 16 and decode_step_input.shape[0] == 2

    def dot(left, right, over):
        return lax.dot_general(left, right, (over, ((), ())), preferred_element_type=f32)

    firsts = jnp.concatenate([gate_first_matrix, up_first_matrix], axis=1)
    inner = jnp.concatenate(
        [
            jnp.dot(training_token_input, firsts, preferred_element_type=f32),
            dot(gate_output_gradient, gate_second_matrix, ((1,), (1,))),
            dot(up_output_gradient, up_second_matrix, ((1,), (1,))),
        ],
        axis=1,
    )
    inner, rows_in = lax.optimization_barrier((inner.astype(bf16), decode_step_input))
    inner = pair_sum(inner).astype(bf16)
    inner_b, inner_a = inner[:, : 2 * rank], inner[:, 2 * rank :]

    columns = gate_weight_base.shape[1]
    group = n_dp // n_tensor
    steps = rows_in.shape[0]
    if kernels:
        theirs = row_share(rows_in, 1 - me)[0]
        arrived = [
            swap(jnp.dot(theirs, weight, preferred_element_type=f32).astype(bf16))
            for weight in (gate_weight_base, up_weight_base)
        ]
        similar = dot(rows_in, training_token_input, ((2,), (1,))).astype(bf16)
        change = dot(similar, inner_a, ((2,), (0,))).astype(bf16)
        block = lax.rem(replica, group)

        def old_block(matrix):
            return lax.dynamic_slice_in_dim(matrix, block * columns, columns, 1)

        seconds, change = new_seconds(
            dot(inner_b[:, :rank], gate_output_gradient, ((0,), (0,))).astype(bf16),
            dot(inner_b[:, rank:], up_output_gradient, ((0,), (0,))).astype(bf16),
            jnp.concatenate([old_block(gate_second_matrix), old_block(up_second_matrix)], axis=0),
            change.reshape(-1, 2 * rank),
            second_learning_rate,
        )
        low = dot(rows_in, firsts, ((2,), (0,))) - first_learning_rate * change.reshape(
            steps, -1, 2 * rank
        ).astype(f32)
    else:
        unit = 16 * n_tensor
        padded = -(-columns // unit) * unit
        piece = padded // n_tensor
        second_gradient = jnp.concatenate(
            [
                dot(gate_output_gradient, inner_b[:, :rank], ((0,), (0,))).astype(bf16),
                dot(up_output_gradient, inner_b[:, rank:], ((0,), (0,))).astype(bf16),
            ],
            axis=1,
        )
        second_gradient = jnp.pad(
            second_gradient.reshape(group, columns, 2 * rank),
            ((0, 0), (0, padded - columns), (0, 0)),
        ).reshape(group * padded, 2 * rank)
        first_gradient = dot(training_token_input, inner_a, ((0,), (0,))).astype(bf16)
        rows_in, second_gradient, first_gradient = lax.optimization_barrier(
            (rows_in, second_gradient, first_gradient)
        )
        second_gradient = lax.psum_scatter(second_gradient, "dp", scatter_dimension=0, tiled=True)
        first_gradient = lax.psum(first_gradient, "dp")
        start = replica // n_tensor * columns + replica % n_tensor * piece

        def old_piece(matrix):
            wide = jnp.pad(matrix, ((0, 0), (0, padded)))
            return lax.dynamic_slice_in_dim(wide, start, piece, 1).T

        old = jnp.concatenate([old_piece(gate_second_matrix), old_piece(up_second_matrix)], axis=1)
        stepped = (
            old.astype(f32) - second_learning_rate * second_gradient.astype(f32)
        ).astype(bf16)
        routes = [
            (
                (block * n_tensor + part) * n_tensor + side,
                (side * group + block) * n_tensor + part,
            )
            for block in range(group)
            for part in range(n_tensor)
            for side in range(n_tensor)
        ]
        stepped = lax.ppermute(stepped, ("dp", "tensor"), routes)
        seconds = lax.all_gather(stepped, "tensor", axis=0, tiled=True)[:columns].T
        new_firsts = (
            firsts.astype(f32) - first_learning_rate * first_gradient.astype(f32)
        ).astype(bf16)
        low = dot(rows_in, new_firsts, ((2,), (0,)))
        low = lax.psum_scatter(
            low.astype(bf16), "tensor", scatter_dimension=1, tiled=True
        ).astype(bf16)

    def base(rows, weight):
        return dot(rows, weight, ((2,), (0,))).astype(bf16)

    weights = (gate_weight_base, up_weight_base)
    if kernels:

        def share_of(side):
            value = row_share(low, side).astype(bf16).reshape(-1, 2 * rank)
            return jnp.stack([value[:, :rank], value[:, rank:]])

        result = decode(
            rows_in.reshape(-1, rows_in.shape[2]),
            gate_weight_base.T,
            up_weight_base.T,
            down_weight_base,
            share_of(me),
            share_of(1 - me),
            seconds.reshape(2, rank, columns),
            *arrived,
            steps,
        )
        return result.reshape(steps, -1, result.shape[1])

    base_sums = [
        lax.psum_scatter(
            base(rows_in, weight), "tensor", scatter_dimension=1, tiled=True
        ).astype(f32)
        for weight in weights
    ]
    gate = base_sums[0] + dot(low[..., :rank], seconds[:rank], ((2,), (0,)))
    upper = base_sums[1] + dot(low[..., rank:], seconds[rank:], ((2,), (0,)))
    hidden = (jax.nn.silu(gate) * upper).astype(bf16)

    hidden = lax.all_gather(hidden, "tensor", axis=1, tiled=True)
    steps, rows, _ = hidden.shape
    out = dot(hidden, down_weight_base, ((2,), (0,))).astype(bf16)
    out = out.reshape(steps * rows, -1)
    out = lax.psum_scatter(out, "dp", scatter_dimension=0, tiled=True)
    out = lax.all_gather(out, "dp", axis=0, tiled=True)
    return out.reshape(steps, rows, -1)


def solution(mesh):
    placed = (
        P("dp", "tensor"),
        P("dp", "tensor"),
        P("dp", "tensor"),
        P("tensor", None),
        P(None, "tensor"),
        P("tensor", None),
        P(None, "tensor"),
        P("tensor", "dp"),
        P("tensor", "dp"),
        P("dp", "tensor"),
        P(None, None, "tensor"),
    )
    return jax.shard_map(
        on_device, mesh=mesh, in_specs=placed, out_specs=P(None, None, "tensor"), check_vma=False
    )
```

profile of v0, /device:TPU:0, one launch (start us, length us, event | category | flops | bytes accessed | tf_op | source)
XLA Modules:
  0.0 312.6 jit_solution(11832348046888544152)
XLA Ops:
  0.0 2.4 copy.17
  2.4 0.0 slice-start
  2.4 2.5 copy.18
  4.9 0.0 slice-start.1
  4.9 0.0 copy-start.1
  4.9 5.3 %convolution_convert_fusion.6 = bf16[256,64]{0,1:T(8,128)(2,1)S(1)} fusion(bf16[64,14784]{1,0:T(8,128)(2,1)} %param.15, bf16[256,14784]{0,1:T(8,128)(2,1)} %param.12), kind=kOutput, calls=%fused_computation.14 | convolution fusion | flops 484458496 | bytes 9494528 | tf_op jit(solution)/shard_map/dot_general | solution.py:597
  10.2 0.0 slice-done
  10.2 0.0 slice-done.1
  10.2 0.2 copy-done.1
  10.4 0.0 copy-start.2
  10.4 0.0 copy-start.4
  10.4 0.0 copy-start.6
  10.4 1.4 convolution_convert_fusion.5
  11.8 0.0 copy-done.2
  11.8 0.1 copy-done.4
  11.9 0.7 copy-done.6
  12.6 0.0 slice-start.2
  12.6 1.3 fusion.11
  14.0 0.7 pad_maximum_fusion.6
  14.7 3.0 collective-permute-start
  17.6 0.0 slice-start.3
  17.6 0.0 slice-start.4
  17.6 0.0 slice-start.5
  17.6 10.4 %convolution_convert_fusion.3 = bf16[256,1848]{0,1:T(8,128)(2,1)} fusion(bf16[4096,1848]{0,1:T(8,128)(2,1)} %param.18, bf16[2,512,4096]{2,1,0:T(8,128)(2,1)} %param.21, s32[]{:T(128)S(6)} %select_n.13), kind=kOutput, calls=%fused_computation.3 | convolution fusion | flops 3876009984 | bytes 18182148 | tf_op jit(solution)/shard_map/dot_general | solution.py:618
  28.1 0.0 collective-permute-start.1
  28.1 0.0 slice-done.2
  28.1 0.0 slice-done.3
  28.1 0.0 slice-done.4
  28.1 0.0 slice-done.5
  28.1 6.7 %convolution_convert_fusion.2 = bf16[256,1848]{0,1:T(8,128)(2,1)} fusion(bf16[4096,1848]{0,1:T(8,128)(2,1)S(1)} %bitcast.57, bf16[2,512,4096]{2,1,0:T(8,128)(2,1)} %param.21, s32[]{:T(128)S(6)} %select_n.13), kind=kOutput, calls=%fused_computation.2 | convolution fusion | flops 3876009984 | bytes 18182148 | tf_op jit(solution)/shard_map/dot_general | solution.py:618
  34.9 2.0 collective-permute-start.2
  36.9 1.2 constant_dynamic-slice_fusion
  38.1 0.0 collective-permute-done
  38.1 1.0 add_convert_fusion
  39.2 6.6 %fusion.8 = bf16[2,512,128]{2,1,0:T(8,128)(2,1)S(1)} fusion(bf16[2,512,4096]{2,1,0:T(8,128)(2,1)} %param.21, bf16[256,4096]{1,0:T(8,128)(2,1)} %param.11, bf16[256,256]{0,1:T(8,128)(2,1)S(1)} %add_convert_fusion), kind=kOutput, calls=%fused_computation.10 | convolution fusion | flops 2214985728 | bytes 10813440 | tf_op jit(solution)/shard_map/dot_general | solution.py:597
  45.7 0.0 slice-start.6
  45.8 5.7 %convolution_convert_fusion.up_ref = bf16[64,14784]{1,0:T(8,128)(2,1)S(1)} fusion(bf16[256,14784]{0,1:T(8,128)(2,1)} %param.13, bf16[256,256]{0,1:T(8,128)(2,1)S(1)} %add_convert_fusion), kind=kOutput, calls=%fused_computation | convolution fusion | flops 485388288 | bytes 9494528 | tf_op jit(solution)/shard_map/dot_general | solution.py:597
  51.5 0.0 slice-start.7
  51.5 0.0 copy-start.3
  51.5 0.0 copy-start.5
  51.5 5.7 %convolution_convert_fusion.1.gate_ref = bf16[64,14784]{1,0:T(8,128)(2,1)S(1)} fusion(bf16[256,14784]{0,1:T(8,128)(2,1)} %param.12, bf16[256,256]{0,1:T(8,128)(2,1)S(1)} %add_convert_fusion), kind=kOutput, calls=%fused_computation.1 | convolution fusion | flops 485388288 | bytes 9494528 | tf_op jit(solution)/shard_map/dot_general | solution.py:597
  57.2 50.1 %seconds.1 = (bf16[128,1848]{1,0:T(8,128)(2,1)S(1)}, bf16[1024,128]{1,0:T(8,128)(2,1)S(1)}) custom-call(bf16[64,14784]{1,0:T(8,128)(2,1)S(1)} %convolution_convert_fusion.1.gate_ref, bf16[64,14784]{1,0:T(8,128)(2,1)S(1)} %convolution_convert_fusion.up_ref, bf16[128,1848]{1,0:T(8,128)(2,1)S(1)} %pad_maximum_fusion.1.old_ref, bf16[1024,128]{1,0:T(8,128)(2,1)S(1)} %bitcast.50), custom_call_target="tpu_custom_call" | custom-call | bytes 100000000 | tf_op jit(solution)/shard_map/seconds/pallas_call | solution.py:545
  107.3 0.0 copy-start
  107.3 0.0 slice-done.6
  107.3 0.0 slice-done.7
  107.4 0.0 copy-done.3
  107.4 0.0 copy-done.5
  107.4 2.4 convolution_subtract_fusion
  109.8 0.0 copy-done
  109.8 0.1 slice_bitcast_fusion.3
  110.0 0.8 pad_maximum_fusion.2.low_ref
  110.7 0.1 slice_bitcast_fusion.1
  110.8 0.8 pad_maximum_fusion.3.pass_ref
  111.6 0.0 collective-permute-done.1
  111.6 1.4 copy.20.first_gate_ref
  113.0 0.0 collective-permute-done.2
  113.0 1.4 copy.21.first_up_ref
  114.4 190.0 %decode.1 = bf16[1024,4096]{1,0:T(8,128)(2,1)} custom-call(bf16[1024,4096]{1,0:T(8,128)(2,1)} %bitcast.58, bf16[1848,4096]{1,0:T(8,128)(2,1)} %bitcast.54, bf16[1848,4096]{1,0:T(8,128)(2,1)} %bitcast.55, bf16[1848,4096]{1,0:T(8,128)(2,1)} %down_ref.1, bf16[2,512,64]{2,1,0:T(8,128)(2,1)} %pad_maximum_fusion.2.low_ref, ...), custom_call_target="tpu_custom_call" | custom-call | tf_op jit(solution)/shard_map/decode/pallas_call | solution.py:346
  304.4 7.9 %copy.25 = bf16[2,512,4096]{2,1,0:T(8,128)(2,1)} copy(bf16[2,512,4096]{2,1,0:T(8,128)(2,1)} %bitcast.53) | data formatting | bytes 16777216
  (6 shorter events, 0.1 us)
Async XLA Ops:
  2.4 7.8 %slice-start = ((s8[7569408]{0:T(1024)(128)(4,1)}), s8[3375104]{0:T(1024)(128)(4,1)S(1)}, s32[]{:S(2)}) async-start(s8[7569408]{0:T(1024)(128)(4,1)} %bitcast.51), calls=%async_computation | async-start | bytes 6750208
  4.9 5.3 %slice-start.1 = ((s8[7569408]{0:T(1024)(128)(4,1)}), s8[4194304]{0:T(1024)(128)(4,1)S(1)}, s32[]{:S(2)}) async-start(s8[7569408]{0:T(1024)(128)(4,1)} %bitcast.51), calls=%async_computation.1 | async-start | bytes 8388608
  4.9 5.5 %copy-start.1 = (bf16[64,14784]{1,0:T(8,128)(2,1)S(1)}, bf16[64,14784]{1,0:T(8,128)(2,1)}, u32[]{:S(2)}) copy-start(bf16[64,14784]{1,0:T(8,128)(2,1)} %param.17) | copy-start | bytes 5677060
  10.4 1.4 copy-start.2
  10.4 1.5 copy-start.4
  10.4 2.2 copy-start.6
  12.6 15.4 %slice-start.2 = ((s8[15138816]{0:T(1024)(128)(4,1)}), s8[2555904]{0:T(1024)(128)(4,1)S(1)}, s32[]{:S(2)}) async-start(s8[15138816]{0:T(1024)(128)(4,1)} %bitcast.56), calls=%async_computation.2 | async-start | bytes 5111808
  14.7 23.5 %collective-permute-start = (bf16[256,256]{0,1:T(8,128)(2,1)}, bf16[256,256]{0,1:T(8,128)(2,1)}, u32[]{:S(2)}, u32[]{:S(2)}) collective-permute-start(bf16[256,256]{0,1:T(8,128)(2,1)} %pad_maximum_fusion.6), channel_id=1, source_target_pairs={{0,1},{1,0},{2,3},{3,2},{4,5},{5,4},{6,7},{7,6},{8,9},{9,8},{10,11... | collective-permute-start | bytes 393224 | tf_op jit(solution)/shard_map/ppermute | solution.py:19
  17.6 10.5 %slice-start.3 = ((s8[15138816]{0:T(1024)(128)(4,1)}), s8[4194304]{0:T(1024)(128)(4,1)S(1)}, s32[]{:S(2)}) async-start(s8[15138816]{0:T(1024)(128)(4,1)} %bitcast.56), calls=%async_computation.3 | async-start | bytes 8388608
  17.6 10.5 %slice-start.4 = ((s8[15138816]{0:T(1024)(128)(4,1)}), s8[4194304]{0:T(1024)(128)(4,1)S(1)}, s32[]{:S(2)}) async-start(s8[15138816]{0:T(1024)(128)(4,1)} %bitcast.56), calls=%async_computation.4 | async-start | bytes 8388608
  17.6 10.5 %slice-start.5 = ((s8[15138816]{0:T(1024)(128)(4,1)}), s8[4194304]{0:T(1024)(128)(4,1)S(1)}, s32[]{:S(2)}) async-start(s8[15138816]{0:T(1024)(128)(4,1)} %bitcast.56), calls=%async_computation.5 | async-start | bytes 8388608
  28.1 83.5 %collective-permute-start.1 = (bf16[256,1848]{0,1:T(8,128)(2,1)}, bf16[256,1848]{0,1:T(8,128)(2,1)S(1)}, u32[]{:S(2)}, u32[]{:S(2)}) collective-permute-start(bf16[256,1848]{0,1:T(8,128)(2,1)} %convolution_convert_fusion.3), channel_id=1, source_target_pairs={{0,1},{1,0},{2,3},{3,2},{4,5},{5,4},{6,7},{7,6},{8,9},{9,8},{10,11... | collective-permute-start | bytes 2838536 | tf_op jit(solution)/shard_map/ppermute | solution.py:19
  34.9 78.1 %collective-permute-start.2 = (bf16[256,1848]{0,1:T(8,128)(2,1)}, bf16[256,1848]{0,1:T(8,128)(2,1)S(1)}, u32[]{:S(2)}, u32[]{:S(2)}) collective-permute-start(bf16[256,1848]{0,1:T(8,128)(2,1)} %convolution_convert_fusion.2), channel_id=1, source_target_pairs={{0,1},{1,0},{2,3},{3,2},{4,5},{5,4},{6,7},{7,6},{8,9},{9,8},{10,11... | collective-permute-start | bytes 2838536 | tf_op jit(solution)/shard_map/ppermute | solution.py:19
  45.7 61.6 %slice-start.6 = ((s8[8388608]{0:T(1024)(128)(4,1)}), s8[4194304]{0:T(1024)(128)(4,1)S(1)}, s32[]{:S(2)}) async-start(s8[8388608]{0:T(1024)(128)(4,1)} %bitcast.59), calls=%async_computation.6 | async-start | bytes 8388608
  51.5 55.9 %slice-start.7 = ((s8[8388608]{0:T(1024)(128)(4,1)}), s8[4194304]{0:T(1024)(128)(4,1)S(1)}, s32[]{:S(2)}) async-start(s8[8388608]{0:T(1024)(128)(4,1)} %bitcast.59), calls=%async_computation.7 | async-start | bytes 8388608
  51.5 55.9 %copy-start.3 = (bf16[4096,64]{1,0:T(8,128)(2,1)S(1)}, bf16[4096,64]{1,0:T(8,128)(2,1)}, u32[]{:S(2)}) copy-start(bf16[4096,64]{1,0:T(8,128)(2,1)} %copy.17) | copy-start | bytes 1572868
  51.5 55.9 %copy-start.5 = (bf16[4096,64]{1,0:T(8,128)(2,1)S(1)}, bf16[4096,64]{1,0:T(8,128)(2,1)}, u32[]{:S(2)}) copy-start(bf16[4096,64]{1,0:T(8,128)(2,1)} %copy.18) | copy-start | bytes 1572868
  107.3 2.5 copy-start
where the time goes:
time: 317 us; the launch traced here: 313 us
  Pallas kernels  240 us (76%)
  matrix products  45.6 us (14%)
  local copies, waits for them, and re-layouts  18.1 us (6%)
  starting transfers between devices  4.99 us (2%)
  other arithmetic  3.29 us (1%)
    pallas_call x1, Pallas kernels, decode(): pl.pallas_call(functools.partial(decode_kernel, n_dp, steps), out_shape=j...  190 us
    pallas_call x1, Pallas kernels, new_seconds(): pl.pallas_call(functools.partial(seconds_kernel, n_dp, n_tensor, rate), o...  50.1 us
    dot_general x6, matrix products, dot(): lax.dot_general(left, right, (over, ((), ())), preferred_element_type=f32)  27.1 us
    dot_general x2, matrix products, on_device(): jnp.dot(theirs, weight, preferred_element_type=f32).astype(bf16)  17.2 us
    unnamed x33, local copies, waits for them, and re-layouts  13.8 us
  transfers between devices with their start and end apart: 3, of which 0 were waited for; matrix products, arithmetic and copies ran while one was open for 14% of the time, Pallas kernels for 16%

commit v1 on v0

--- a/solution.py
+++ b/solution.py
@@ -276,7 +276,7 @@
     hidden(1)
     for _ in base(1):
         pass
-    for copy in partial_copies(2):
+    for copy in partial_copies(2) + partial_copies(3):
         copy.start()
     weight_load.wait()
     for _ in project(0):
@@ -289,30 +289,22 @@
                 yield
 
     def background():
-        yield
-        for _ in project(1):
-            pass
+        yield from paced(base(2), 6)
+        yield from paced(project(1), 3)
         live[1] = spread(1)
         yield
-        yield from paced(base(2), 6)
         for copy in partial_copies(2):
             copy.wait_recv()
         hidden(2)
-        for copy in partial_copies(3):
-            copy.start()
         yield
-        yield
-        yield from paced(project(2), 4)
+        yield from paced(project(2), 3)
         live[2] = spread(2)
-        yield
         yield
         for copy in partial_copies(3):
             copy.wait_recv()
         hidden(3)
         yield
-        yield
-        for _ in project(3):
-            pass
+        yield from paced(project(3), 3)
         live[3] = spread(3)
 
     rest = background()

time: 317 us -> 319 us (level)
  no operation moved by 1% of the time
where the time goes in v1:
time: 319 us; the launch traced here: 315 us
  Pallas kernels  242 us (76%)
  matrix products  45.6 us (14%)
  local copies, waits for them, and re-layouts  18.1 us (6%)
  starting transfers between devices  4.99 us (2%)
  other arithmetic  3.29 us (1%)
    pallas_call x1, Pallas kernels, decode(): pl.pallas_call(functools.partial(decode_kernel, n_dp, steps), out_shape=j...  192 us
    pallas_call x1, Pallas kernels, new_seconds(): pl.pallas_call(functools.partial(seconds_kernel, n_dp, n_tensor, rate), o...  50.1 us
    dot_general x6, matrix products, dot(): lax.dot_general(left, right, (over, ((), ())), preferred_element_type=f32)  27.1 us
    dot_general x2, matrix products, on_device(): jnp.dot(theirs, weight, preferred_element_type=f32).astype(bf16)  17.2 us
    unnamed x33, local copies, waits for them, and re-layouts  13.8 us
  transfers between devices with their start and end apart: 3, of which 0 were waited for; matrix products, arithmetic and copies ran while one was open for 14% of the time, Pallas kernels for 16%

profile of v1, /device:TPU:0, one launch (start us, length us, event | category | flops | bytes accessed | tf_op | source)
XLA Modules:
  0.0 314.6 jit_solution(4350309089929267326)
XLA Ops:
  0.0 2.4 copy.17
  2.4 0.0 slice-start
  2.4 2.5 copy.18
  4.9 0.0 slice-start.1
  4.9 0.0 copy-start.1
  4.9 5.3 %convolution_convert_fusion.6 = bf16[256,64]{0,1:T(8,128)(2,1)S(1)} fusion(bf16[64,14784]{1,0:T(8,128)(2,1)} %param.15, bf16[256,14784]{0,1:T(8,128)(2,1)} %param.12), kind=kOutput, calls=%fused_computation.14 | convolution fusion | flops 484458496 | bytes 9494528 | tf_op jit(solution)/shard_map/dot_general | solution.py:589
  10.2 0.0 slice-done
  10.2 0.0 slice-done.1
  10.2 0.2 copy-done.1
  10.4 0.0 copy-start.2
  10.4 0.0 copy-start.4
  10.4 0.0 copy-start.6
  10.4 1.4 convolution_convert_fusion.5
  11.8 0.0 copy-done.2
  11.8 0.1 copy-done.4
  11.9 0.7 copy-done.6
  12.6 0.0 slice-start.2
  12.6 1.3 fusion.11
  14.0 0.7 pad_maximum_fusion.6
  14.7 3.0 collective-permute-start
  17.6 0.0 slice-start.3
  17.6 0.0 slice-start.4
  17.6 0.0 slice-start.5
  17.6 10.4 %convolution_convert_fusion.3 = bf16[256,1848]{0,1:T(8,128)(2,1)} fusion(bf16[4096,1848]{0,1:T(8,128)(2,1)} %param.18, bf16[2,512,4096]{2,1,0:T(8,128)(2,1)} %param.21, s32[]{:T(128)S(6)} %select_n.13), kind=kOutput, calls=%fused_computation.3 | convolution fusion | flops 3876009984 | bytes 18182148 | tf_op jit(solution)/shard_map/dot_general | solution.py:610
  28.1 0.0 collective-permute-start.1
  28.1 0.0 slice-done.2
  28.1 0.0 slice-done.3
  28.1 0.0 slice-done.4
  28.1 0.0 slice-done.5
  28.1 6.7 %convolution_convert_fusion.2 = bf16[256,1848]{0,1:T(8,128)(2,1)} fusion(bf16[4096,1848]{0,1:T(8,128)(2,1)S(1)} %bitcast.57, bf16[2,512,4096]{2,1,0:T(8,128)(2,1)} %param.21, s32[]{:T(128)S(6)} %select_n.13), kind=kOutput, calls=%fused_computation.2 | convolution fusion | flops 3876009984 | bytes 18182148 | tf_op jit(solution)/shard_map/dot_general | solution.py:610
  34.9 2.0 collective-permute-start.2
  36.9 1.2 constant_dynamic-slice_fusion
  38.1 0.0 collective-permute-done
  38.1 1.0 add_convert_fusion
  39.2 6.6 %fusion.8 = bf16[2,512,128]{2,1,0:T(8,128)(2,1)S(1)} fusion(bf16[2,512,4096]{2,1,0:T(8,128)(2,1)} %param.21, bf16[256,4096]{1,0:T(8,128)(2,1)} %param.11, bf16[256,256]{0,1:T(8,128)(2,1)S(1)} %add_convert_fusion), kind=kOutput, calls=%fused_computation.10 | convolution fusion | flops 2214985728 | bytes 10813440 | tf_op jit(solution)/shard_map/dot_general | solution.py:589
  45.7 0.0 slice-start.6
  45.8 5.7 %convolution_convert_fusion.up_ref = bf16[64,14784]{1,0:T(8,128)(2,1)S(1)} fusion(bf16[256,14784]{0,1:T(8,128)(2,1)} %param.13, bf16[256,256]{0,1:T(8,128)(2,1)S(1)} %add_convert_fusion), kind=kOutput, calls=%fused_computation | convolution fusion | flops 485388288 | bytes 9494528 | tf_op jit(solution)/shard_map/dot_general | solution.py:589
  51.5 0.0 slice-start.7
  51.5 0.0 copy-start.3
  51.5 0.0 copy-start.5
  51.5 5.7 %convolution_convert_fusion.1.gate_ref = bf16[64,14784]{1,0:T(8,128)(2,1)S(1)} fusion(bf16[256,14784]{0,1:T(8,128)(2,1)} %param.12, bf16[256,256]{0,1:T(8,128)(2,1)S(1)} %add_convert_fusion), kind=kOutput, calls=%fused_computation.1 | convolution fusion | flops 485388288 | bytes 9494528 | tf_op jit(solution)/shard_map/dot_general | solution.py:589
  57.2 50.1 %seconds.1 = (bf16[128,1848]{1,0:T(8,128)(2,1)S(1)}, bf16[1024,128]{1,0:T(8,128)(2,1)S(1)}) custom-call(bf16[64,14784]{1,0:T(8,128)(2,1)S(1)} %convolution_convert_fusion.1.gate_ref, bf16[64,14784]{1,0:T(8,128)(2,1)S(1)} %convolution_convert_fusion.up_ref, bf16[128,1848]{1,0:T(8,128)(2,1)S(1)} %pad_maximum_fusion.1.old_ref, bf16[1024,128]{1,0:T(8,128)(2,1)S(1)} %bitcast.50), custom_call_target="tpu_custom_call" | custom-call | bytes 100000000 | tf_op jit(solution)/shard_map/seconds/pallas_call | solution.py:537
  107.3 0.0 copy-start
  107.3 0.0 slice-done.6
  107.3 0.0 slice-done.7
  107.4 0.0 copy-done.3
  107.4 0.0 copy-done.5
  107.4 2.4 convolution_subtract_fusion
  109.8 0.0 copy-done
  109.8 0.1 slice_bitcast_fusion.3
  110.0 0.8 pad_maximum_fusion.2.low_ref
  110.7 0.1 slice_bitcast_fusion.1
  110.8 0.8 pad_maximum_fusion.3.pass_ref
  111.6 0.0 collective-permute-done.1
  111.6 1.4 copy.20.first_gate_ref
  113.0 0.0 collective-permute-done.2
  113.0 1.4 copy.21.first_up_ref
  114.4 192.0 %decode.1 = bf16[1024,4096]{1,0:T(8,128)(2,1)} custom-call(bf16[1024,4096]{1,0:T(8,128)(2,1)} %bitcast.58, bf16[1848,4096]{1,0:T(8,128)(2,1)} %bitcast.54, bf16[1848,4096]{1,0:T(8,128)(2,1)} %bitcast.55, bf16[1848,4096]{1,0:T(8,128)(2,1)} %down_ref.1, bf16[2,512,64]{2,1,0:T(8,128)(2,1)} %pad_maximum_fusion.2.low_ref, ...), custom_call_target="tpu_custom_call" | custom-call | tf_op jit(solution)/shard_map/decode/pallas_call | solution.py:338
  306.5 7.9 %copy.25 = bf16[2,512,4096]{2,1,0:T(8,128)(2,1)} copy(bf16[2,512,4096]{2,1,0:T(8,128)(2,1)} %bitcast.53) | data formatting | bytes 16777216
  (6 shorter events, 0.1 us)
Async XLA Ops:
  2.4 7.8 %slice-start = ((s8[7569408]{0:T(1024)(128)(4,1)}), s8[3375104]{0:T(1024)(128)(4,1)S(1)}, s32[]{:S(2)}) async-start(s8[7569408]{0:T(1024)(128)(4,1)} %bitcast.51), calls=%async_computation | async-start | bytes 6750208
  4.9 5.3 %slice-start.1 = ((s8[7569408]{0:T(1024)(128)(4,1)}), s8[4194304]{0:T(1024)(128)(4,1)S(1)}, s32[]{:S(2)}) async-start(s8[7569408]{0:T(1024)(128)(4,1)} %bitcast.51), calls=%async_computation.1 | async-start | bytes 8388608
  4.9 5.5 %copy-start.1 = (bf16[64,14784]{1,0:T(8,128)(2,1)S(1)}, bf16[64,14784]{1,0:T(8,128)(2,1)}, u32[]{:S(2)}) copy-start(bf16[64,14784]{1,0:T(8,128)(2,1)} %param.17) | copy-start | bytes 5677060
  10.4 1.4 copy-start.2
  10.4 1.5 copy-start.4
  10.4 2.2 copy-start.6
  12.6 15.4 %slice-start.2 = ((s8[15138816]{0:T(1024)(128)(4,1)}), s8[2555904]{0:T(1024)(128)(4,1)S(1)}, s32[]{:S(2)}) async-start(s8[15138816]{0:T(1024)(128)(4,1)} %bitcast.56), calls=%async_computation.2 | async-start | bytes 5111808
  14.7 23.5 %collective-permute-start = (bf16[256,256]{0,1:T(8,128)(2,1)}, bf16[256,256]{0,1:T(8,128)(2,1)}, u32[]{:S(2)}, u32[]{:S(2)}) collective-permute-start(bf16[256,256]{0,1:T(8,128)(2,1)} %pad_maximum_fusion.6), channel_id=1, source_target_pairs={{0,1},{1,0},{2,3},{3,2},{4,5},{5,4},{6,7},{7,6},{8,9},{9,8},{10,11... | collective-permute-start | bytes 393224 | tf_op jit(solution)/shard_map/ppermute | solution.py:19
  17.6 10.5 %slice-start.3 = ((s8[15138816]{0:T(1024)(128)(4,1)}), s8[4194304]{0:T(1024)(128)(4,1)S(1)}, s32[]{:S(2)}) async-start(s8[15138816]{0:T(1024)(128)(4,1)} %bitcast.56), calls=%async_computation.3 | async-start | bytes 8388608
  17.6 10.5 %slice-start.4 = ((s8[15138816]{0:T(1024)(128)(4,1)}), s8[4194304]{0:T(1024)(128)(4,1)S(1)}, s32[]{:S(2)}) async-start(s8[15138816]{0:T(1024)(128)(4,1)} %bitcast.56), calls=%async_computation.4 | async-start | bytes 8388608
  17.6 10.5 %slice-start.5 = ((s8[15138816]{0:T(1024)(128)(4,1)}), s8[4194304]{0:T(1024)(128)(4,1)S(1)}, s32[]{:S(2)}) async-start(s8[15138816]{0:T(1024)(128)(4,1)} %bitcast.56), calls=%async_computation.5 | async-start | bytes 8388608
  28.1 83.5 %collective-permute-start.1 = (bf16[256,1848]{0,1:T(8,128)(2,1)}, bf16[256,1848]{0,1:T(8,128)(2,1)S(1)}, u32[]{:S(2)}, u32[]{:S(2)}) collective-permute-start(bf16[256,1848]{0,1:T(8,128)(2,1)} %convolution_convert_fusion.3), channel_id=1, source_target_pairs={{0,1},{1,0},{2,3},{3,2},{4,5},{5,4},{6,7},{7,6},{8,9},{9,8},{10,11... | collective-permute-start | bytes 2838536 | tf_op jit(solution)/shard_map/ppermute | solution.py:19
  34.9 78.1 %collective-permute-start.2 = (bf16[256,1848]{0,1:T(8,128)(2,1)}, bf16[256,1848]{0,1:T(8,128)(2,1)S(1)}, u32[]{:S(2)}, u32[]{:S(2)}) collective-permute-start(bf16[256,1848]{0,1:T(8,128)(2,1)} %convolution_convert_fusion.2), channel_id=1, source_target_pairs={{0,1},{1,0},{2,3},{3,2},{4,5},{5,4},{6,7},{7,6},{8,9},{9,8},{10,11... | collective-permute-start | bytes 2838536 | tf_op jit(solution)/shard_map/ppermute | solution.py:19
  45.7 61.6 %slice-start.6 = ((s8[8388608]{0:T(1024)(128)(4,1)}), s8[4194304]{0:T(1024)(128)(4,1)S(1)}, s32[]{:S(2)}) async-start(s8[8388608]{0:T(1024)(128)(4,1)} %bitcast.59), calls=%async_computation.6 | async-start | bytes 8388608
  51.5 55.9 %slice-start.7 = ((s8[8388608]{0:T(1024)(128)(4,1)}), s8[4194304]{0:T(1024)(128)(4,1)S(1)}, s32[]{:S(2)}) async-start(s8[8388608]{0:T(1024)(128)(4,1)} %bitcast.59), calls=%async_computation.7 | async-start | bytes 8388608
  51.5 55.9 %copy-start.3 = (bf16[4096,64]{1,0:T(8,128)(2,1)S(1)}, bf16[4096,64]{1,0:T(8,128)(2,1)}, u32[]{:S(2)}) copy-start(bf16[4096,64]{1,0:T(8,128)(2,1)} %copy.17) | copy-start | bytes 1572868
  51.5 55.9 %copy-start.5 = (bf16[4096,64]{1,0:T(8,128)(2,1)S(1)}, bf16[4096,64]{1,0:T(8,128)(2,1)}, u32[]{:S(2)}) copy-start(bf16[4096,64]{1,0:T(8,128)(2,1)} %copy.18) | copy-start | bytes 1572868
  107.3 2.5 copy-start
